TPU v7x, 8 devices: a whole 2x2x1 slice. The times are simulated.
8 devices in a mesh: dp: 4 (over z, y, x), tp: 2 (over core).
Axes of the slice: x: 2, y: 2, z: 1, core: 2. Of those that a mesh axis runs over, the one named last changes fastest.
Arguments:
- w_up: bfloat16 [2, 1536, 8960], P(None, None, 'tp')
- w_down: bfloat16 [2, 8960, 1536], P(None, 'tp')
- x_saved: bfloat16 [2, 4, 4096, 1536], P(None, 'dp')
- h_saved: bfloat16 [2, 4, 4096, 8960], P(None, 'dp', None, 'tp')
- grad_out: bfloat16 [4, 4096, 1536], P('dp')
Outputs:
- output 1: bfloat16 [4, 4096, 1536], P('dp')
- output 2: float32 [2, 1536, 8960], P(None, None, 'tp')
- output 3: float32 [2, 8960, 1536], P(None, 'tp')
All inputs are finite; a program needn't handle non-finite values.
Results may differ from a plain program's by a relative error of at most 0.011775.
Values are sent between devices in bfloat16 or wider.
A program may use at most 1.25 GiB of HBM per device.

v0:
```python
import jax
import jax.numpy as jnp
from jax import lax
from jax.sharding import PartitionSpec as P


def gelu_parts(hidden):
    tanh_val = jnp.tanh(0.7978845608028654 * (hidden + 0.044715 * hidden * hidden * hidden))
    gelu_out = 0.5 * hidden * (1.0 + tanh_val)
    gelu_slope = 0.5 * (1.0 + tanh_val) + 0.5 * hidden * (1.0 - tanh_val * tanh_val) * 0.7978845608028654 * (1.0 + 0.134145 * hidden * hidden)
    return gelu_out, gelu_slope


def solution(mesh):
    def run_backward(w_up, w_down, x_saved, h_saved, grad_out):
        layer_count = w_up.shape[0]
        grad_cur = grad_out
        up_grads = {}
        down_grads = {}
        for layer_idx in reversed(range(layer_count)):
            gelu_out, gelu_slope = gelu_parts(h_saved[layer_idx].astype(jnp.float32))
            act_grad = jnp.einsum("bsd,fd->bsf", grad_cur, w_down[layer_idx], preferred_element_type=jnp.float32)
            hid_grad = (act_grad * gelu_slope).astype(jnp.bfloat16)
            part_sum = jnp.einsum("bsf,df->bsd", hid_grad, w_up[layer_idx], preferred_element_type=jnp.float32).astype(jnp.bfloat16)
            full_sum = lax.psum(part_sum, "tp")
            down_grads[layer_idx] = jnp.einsum("bsf,bsd->fd", gelu_out.astype(jnp.bfloat16), grad_cur, preferred_element_type=jnp.float32)
            up_grads[layer_idx] = jnp.einsum("bsd,bsf->df", x_saved[layer_idx], hid_grad, preferred_element_type=jnp.float32)
            grad_cur = (grad_cur.astype(jnp.float32) + full_sum.astype(jnp.float32)).astype(jnp.bfloat16)
        up_total = lax.psum(jnp.stack([up_grads[layer_idx] for layer_idx in range(layer_count)]), "dp")
        down_total = lax.psum(jnp.stack([down_grads[layer_idx] for layer_idx in range(layer_count)]), "dp")
        return grad_cur, up_total, down_total
    return jax.shard_map(run_backward, mesh=mesh, in_specs=(P(None, None, "tp"), P(None, "tp", None), P(None, "dp", None, None), P(None, "dp", None, "tp"), P("dp", None, None)), out_specs=(P("dp", None, None), P(None, None, "tp"), P(None, "tp", None)), check_vma=False)
```

profile of v0, /device:TPU:0, one launch (start us, length us, event | category | flops | bytes accessed | tf_op | source)
XLA Modules:
  0.0 2649.5 jit_solution(8567965114980495432)
XLA Ops:
  7.2 0.0 all-reduce.5.cloned.1.call-start
  7.2 126.5 %fusion.21 = bf16[4096,4480]{1,0:T(8,128)(2,1)} fusion(bf16[2,1,4096,4480]{3,2,1,0:T(8,128)(2,1)} %param.8, bf16[2,4480,1536]{2,1,0:T(8,128)(2,1)} %param.6, bf16[1,4096,1536]{2,1,0:T(8,128)(2,1)} %param.9), kind=kOutput, calls=%fused_computation.33 | convolution fusion | flops 56738447360 | bytes 99745792 | tf_op jit(solution)/shard_map/bsd,fd->bsf/dot_general | solution.py:22
  133.7 67.4 %fusion.64 = bf16[1,4096,1536]{2,1,0:T(8,128)(2,1)} fusion(bf16[4096,4480]{1,0:T(8,128)(2,1)} %fusion.21, bf16[2,1536,4480]{2,1,0:T(8,128)(2,1)} %param.5), kind=kOutput, calls=%fused_computation.78 | convolution fusion | flops 56377737216 | bytes 63045632 | tf_op jit(solution)/shard_map/bsf,df->bsd/dot_general | solution.py:24
  201.2 0.0 all-reduce.5.cloned.1.call-update
  201.2 0.0 all-reduce.7.cloned.1.call-start
  201.2 67.4 %convolution_bitcast_fusion = f32[1,1536,4480]{1,2,0:T(8,128)} fusion(bf16[4096,4480]{1,0:T(8,128)(2,1)} %fusion.21, bf16[2,1,4096,1536]{3,2,1,0:T(8,128)(2,1)} %param.7), kind=kOutput, calls=%fused_computation.66 | convolution fusion | flops 56371445760 | bytes 76808192 | tf_op jit(solution)/shard_map/bsd,bsf->df/dot_general | solution.py:27
  268.7 80.5 %fusion.53 = f32[1,4480,1536]{2,1,0:T(8,128)} fusion(bf16[2,1,4096,4480]{3,2,1,0:T(8,128)(2,1)} %param.8, bf16[1,4096,1536]{2,1,0:T(8,128)(2,1)} %param.9), kind=kOutput, calls=%fused_computation.65 | convolution fusion | flops 56554946560 | bytes 76808192 | tf_op jit(solution)/shard_map/bsf,bsd->fd/dot_general | solution.py:26
  349.2 0.0 all-reduce.5.cloned.1.call-done
  349.2 103.3 %fusion.35 = bf16[4096,4480]{1,0:T(8,128)(2,1)} fusion(bf16[2,1,4096,4480]{3,2,1,0:T(8,128)(2,1)} %param.8, bf16[2,4480,1536]{2,1,0:T(8,128)(2,1)} %param.6, bf16[1,4096,1536]{2,1,0:T(8,128)(2,1)} %all-reduce.5.cloned.1.call-done, bf16[1,4096,1536]{2,1,0:T(8,128)(2,1)} %param.9), kind=kOutput, calls=%fused_computation.47 | convolution fusion | flops 56763613184 | bytes 112328704 | tf_op jit(solution)/shard_map/bsd,fd->bsf/dot_general | solution.py:22
  452.4 67.4 %fusion.67 = bf16[1,4096,1536]{2,1,0:T(8,128)(2,1)} fusion(bf16[4096,4480]{1,0:T(8,128)(2,1)} %fusion.35, bf16[2,1536,4480]{2,1,0:T(8,128)(2,1)} %param.5), kind=kOutput, calls=%fused_computation.79 | convolution fusion | flops 56377737216 | bytes 63045632 | tf_op jit(solution)/shard_map/bsf,df->bsd/dot_general | solution.py:24
  519.8 0.0 all-reduce.7.cloned.1.call-update
  519.9 0.0 all-reduce.9.cloned.1.call-start
  519.9 89.9 %fusion.50 = f32[1,4480,1536]{2,1,0:T(8,128)} fusion(bf16[2,1,4096,4480]{3,2,1,0:T(8,128)(2,1)} %param.8, bf16[1,4096,1536]{2,1,0:T(8,128)(2,1)} %all-reduce.5.cloned.1.call-done, bf16[1,4096,1536]{2,1,0:T(8,128)(2,1)} %param.9), kind=kOutput, calls=%fused_computation.64 | convolution fusion | flops 56580112384 | bytes 89391104 | tf_op jit(solution)/shard_map/bsf,bsd->fd/dot_general | solution.py:26
  609.8 37.4 %pad_maximum_fusion.1 = f32[2,4480,1536]{2,1,0:T(8,128)} fusion(f32[1,4480,1536]{2,1,0:T(8,128)} %fusion.53, f32[1,4480,1536]{2,1,0:T(8,128)} %fusion.50), kind=kLoop, calls=%fused_computation.55 | loop fusion | flops 13762560 | bytes 110100480 | tf_op jit(solution)/shard_map/stack | solution.py:30
  647.2 67.7 %convolution_bitcast_fusion.1 = f32[1,1536,4480]{1,2,0:T(8,128)} fusion(bf16[4096,4480]{1,0:T(8,128)(2,1)} %fusion.35, bf16[2,1,4096,1536]{3,2,1,0:T(8,128)(2,1)} %param.7), kind=kOutput, calls=%fused_computation.67 | convolution fusion | flops 56371445760 | bytes 76808192 | tf_op jit(solution)/shard_map/bsd,bsf->df/dot_general | solution.py:27
  714.9 37.4 %pad_maximum_fusion = f32[2,1536,4480]{1,2,0:T(8,128)} fusion(f32[1,1536,4480]{1,2,0:T(8,128)} %convolution_bitcast_fusion, f32[1,1536,4480]{1,2,0:T(8,128)} %convolution_bitcast_fusion.1), kind=kLoop, calls=%fused_computation.54 | loop fusion | flops 13762560 | bytes 110100480 | tf_op jit(solution)/shard_map/stack | solution.py:29
  752.2 0.0 all-reduce.9.cloned.1.call-update
  752.3 0.0 all-reduce.7.cloned.1.call-done
  752.3 17.8 add_convert_fusion
  770.1 1780.8 %all-reduce.9.cloned.1.call-done = (f32[2,1536,4480]{1,2,0:T(8,128)}, f32[2,4480,1536]{2,1,0:T(8,128)}) async-done(((f32[2,1536,4480]{1,2,0:T(8,128)}, f32[2,4480,1536]{2,1,0:T(8,128)}), (f32[2,1536,4480]{1,2,0:T(8,128)}, f32[2,4480,1536]{2,1,0:T(8,128)})) %all-reduce.9.cloned.1.call-update) | async-done | bytes 110100496 | tf_op jit(solution)/shard_map/psum | solution.py:29
  2550.8 54.3 %copy.8 = f32[2,1536,4480]{2,1,0:T(8,128)} copy(f32[2,1536,4480]{1,2,0:T(8,128)} %get-tuple-element.6) | data formatting | bytes 110100480
  2605.1 37.4 %copy.13 = f32[2,4480,1536]{2,1,0:T(8,128)} copy(f32[2,4480,1536]{2,1,0:T(8,128)} %get-tuple-element.10) | data formatting | bytes 110100480
Async XLA Ops:
  7.2 342.0 %all-reduce.5.cloned.1.call-start = ((), (), s32[]{:S(2)}) async-start(), calls=%async_computation | async-start | bytes 25165824 | tf_op jit(solution)/shard_map/psum | solution.py:25
  201.2 551.1 %all-reduce.7.cloned.1.call-start = ((), (), s32[]{:S(2)}) async-start(), calls=%async_computation.1 | async-start | bytes 25165824 | tf_op jit(solution)/shard_map/psum | solution.py:25
  519.9 2030.9 %all-reduce.9.cloned.1.call-start = ((), (), s32[]{:S(2)}) async-start(), calls=%async_computation.2 | async-start | bytes 220200960 | tf_op jit(solution)/shard_map/psum | solution.py:29
Sparse Core Ops, SparseCore 0:
  201.3 42.4 all-reduce.4
  520.0 42.4 all-reduce.6
  752.4 1798.3 all-reduce.8
where the time goes:
time: 2660 us; the launch traced here: 2650 us
  waiting for transfers between devices  1780 us (67%)
  matrix products  670 us (25%)
  other arithmetic  92.5 us (3%)
  local copies, waits for them, and re-layouts  91.7 us (3%)
    psum x1, waiting for transfers between devices, run_backward(): lax.psum(jnp.stack([up_grads[layer_idx] for layer_idx in range(layer_coun...  1780 us
    dot_general x2, matrix products, run_backward(): jnp.einsum('bsd,fd->bsf', grad_cur, w_down[layer_idx], preferred_element_...  230 us
    dot_general x2, matrix products, run_backward(): jnp.einsum('bsf,bsd->fd', gelu_out.astype(jnp.bfloat16), grad_cur, prefer...  170 us
    dot_general x2, matrix products, run_backward(): jnp.einsum('bsd,bsf->df', x_saved[layer_idx], hid_grad, preferred_element...  135 us
    dot_general x2, matrix products, run_backward(): jnp.einsum('bsf,df->bsd', hid_grad, w_up[layer_idx], preferred_element_ty...  135 us
    unnamed x2, local copies, waits for them, and re-layouts  91.7 us
  transfers between devices with their start and end apart: 3, of which 1 were waited for; matrix products, arithmetic and copies ran while one was open for 15% of the time, Pallas kernels for 0%

commit v1 on v0

v1 whole, which is shorter than its diff:
```python
import functools

import jax
import jax.numpy as jnp
from jax import lax
from jax.experimental import pallas as pl
from jax.experimental.pallas import tpu as pltpu
from jax.sharding import PartitionSpec as P


D = 1536
F = 4480
TOKENS = 4096
QUARTER = 1120
C0 = 0.7978845608028654
NT = (((1,), (1,)), ((), ()))
VMEM_LIMIT = 67043328
ANY = pl.BlockSpec(memory_space=pl.ANY)


def gelu_pair(hidden):
    sq = hidden * hidden
    tanh_val = jnp.tanh(hidden * (C0 + (C0 * 0.044715) * sq))
    p = 0.5 + 0.5 * tanh_val
    gelu_out = hidden * p
    slope = p + (gelu_out * (1.0 - p)) * (2 * C0 + (2 * C0 * 0.134145) * sq)
    return gelu_out, slope


def dot32(a, b, dims=None):
    if dims is None:
        return jnp.dot(a, b, preferred_element_type=jnp.float32)
    return lax.dot_general(a, b, dims, preferred_element_type=jnp.float32)


def rows_of(ref, sel, start, size):
    rows = pl.ds(start, size)
    return ref.at[rows, :] if not sel else ref.at[(*sel, rows, slice(None))]


def chain_body(sub, nsub, nf, emit_w1t, g_ref, h_ref, w1_ref, w2_ref, at_ref, dht_ref, p_ref, *rest):
    w1t_ref = rest[0] if emit_w1t else None
    pacc, das, hts = rest[-3:]
    t, f = pl.program_id(0), pl.program_id(1)

    @pl.when(f == 0)
    def _():
        pacc[...] = jnp.zeros_like(pacc)

    if emit_w1t:

        @pl.when(t == 0)
        def _():
            w1t_ref[...] = w1_ref[...].T

    def first(i):
        das[i] = dot32(w2_ref[...], g_ref[pl.ds(i * sub, sub), :], NT)
        hts[i] = h_ref[pl.ds(i * sub, sub), :].T

    def second(i):
        gelu_out, slope = gelu_pair(hts[i].astype(jnp.float32))
        at_ref[:, pl.ds(i * sub, sub)] = gelu_out.astype(jnp.bfloat16)
        dht_ref[:, pl.ds(i * sub, sub)] = (das[i] * slope).astype(jnp.bfloat16)

    def third(i):
        cols = pl.ds(i * sub, sub)
        pacc[:, cols] += dot32(w1_ref[...], dht_ref[:, cols])

    first(0)
    for i in range(nsub):
        if i + 1 < nsub:
            first(i + 1)
        second(i)
        if i > 0:
            third(i - 1)
    third(nsub - 1)

    @pl.when(f == nf - 1)
    def _():
        p_ref[...] = pacc[...].T.astype(jnp.bfloat16)


def chain(grad, h_saved, w_up, w_down, layer, emit_w1t=False, fc=640, tb=1024, sub=512):
    nt, nf, nsub = TOKENS // tb, F // fc, tb // sub
    col = pl.BlockSpec((fc, tb), lambda t, f: (f, t))
    out_specs = [col, col, pl.BlockSpec((tb, D), lambda t, f: (t, 0))]
    out_shape = [(F, TOKENS), (F, TOKENS), (TOKENS, D)]
    if emit_w1t:
        out_specs.append(pl.BlockSpec((fc, D), lambda t, f: (jnp.where(t == 0, f, nf - 1), 0)))
        out_shape.append((F, D))
    return pl.pallas_call(
        functools.partial(chain_body, sub, nsub, nf, emit_w1t),
        grid=(nt, nf),
        in_specs=[
            pl.BlockSpec((tb, D), lambda t, f: (t, 0)),
            pl.BlockSpec((None, None, tb, fc), lambda t, f: (layer, 0, t, f)),
            pl.BlockSpec((None, D, fc), lambda t, f: (layer, 0, f)),
            pl.BlockSpec((None, fc, D), lambda t, f: (layer, f, 0)),
        ],
        out_specs=out_specs,
        out_shape=[jax.ShapeDtypeStruct(s, jnp.bfloat16) for s in out_shape],
        scratch_shapes=[
            pltpu.VMEM((D, tb), jnp.float32),
            pltpu.VMEM((nsub, fc, sub), jnp.float32),
            pltpu.VMEM((nsub, fc, sub), jnp.bfloat16),
        ],
        compiler_params=pltpu.CompilerParams(
            dimension_semantics=("arbitrary", "arbitrary"), vmem_limit_bytes=VMEM_LIMIT
        ),
        cost_estimate=pl.CostEstimate(flops=4 * TOKENS * D * F, bytes_accessed=6 * TOKENS * F, transcendentals=0),
    )(grad, h_saved, w_up, w_down)


def wgrad_body(cfg, *refs):
    fc, nf, tb, sub, nt = cfg["fc"], cfg["nf"], cfg["tb"], cfg["sub"], cfg["nt"]
    n_own, n_oth, srcs = cfg["n_own"], cfg["n_oth"], cfg["srcs"]
    transpose_out, layer = cfg["transpose_out"], cfg["out_layer"]
    nsub = tb // sub
    it = iter(refs)
    next(it)
    if n_own:
        at_ref, dht_ref = next(it), next(it)
    if n_oth:
        w1_ref, w2_ref = next(it), next(it)
    arrays = [next(it) for _ in range(cfg["n_arrays"])]
    acc_in = (next(it), next(it)) if cfg["acc_in"] else None
    o1, o2, xb, gb, acc1, acc2, xg_sem, in_sem, out_sem = (next(it) for _ in range(9))
    stage = next(it) if transpose_out else None
    w1t = next(it) if cfg["w1_transpose"] and n_oth else None
    if n_oth:
        hs, das, ats, dhs = (next(it) for _ in range(4))
    f, t = pl.program_id(0), pl.program_id(1)
    step = f * nt + t
    slot, fs = lax.rem(step, 2), lax.rem(f, 2)

    def start_xg(tt, sl):
        base = 0
        for xi, xsel, xrow, gi, gsel, grow, n in srcs:
            k = n // tb

            @pl.when((tt >= base) & (tt < base + k))
            def _(base=base, xi=xi, xsel=xsel, xrow=xrow, gi=gi, gsel=gsel, grow=grow):
                r = (tt - base) * tb
                xs = rows_of(arrays[xi], xsel, pl.multiple_of(xrow + r, tb), tb)
                gs = rows_of(arrays[gi], gsel, pl.multiple_of(grow + r, tb), tb)
                pltpu.make_async_copy(xs, xb.at[sl], xg_sem.at[0, sl]).start()
                pltpu.make_async_copy(gs, gb.at[sl], xg_sem.at[1, sl]).start()

            base += k

    def wait_xg(sl):
        pltpu.make_async_copy(xb.at[sl], xb.at[sl], xg_sem.at[0, sl]).wait()
        pltpu.make_async_copy(gb.at[sl], gb.at[sl], xg_sem.at[1, sl]).wait()

    def in_copies(ff, sl):
        rows = pl.ds(pl.multiple_of(ff * fc, 8), fc)
        return (
            pltpu.make_async_copy(acc_in[0].at[rows, :], acc1.at[sl], in_sem.at[0, sl]),
            pltpu.make_async_copy(acc_in[1].at[rows, :], acc2.at[sl], in_sem.at[1, sl]),
        )

    def out1(ff, sl):
        if transpose_out:
            cols = pl.ds(pl.multiple_of(ff * fc, 128), fc)
            return pltpu.make_async_copy(stage, o1.at[layer, :, cols], out_sem.at[0, 0])
        rows = pl.ds(pl.multiple_of(ff * fc, 8), fc)
        return pltpu.make_async_copy(acc1.at[sl], o1.at[rows, :], out_sem.at[0, sl])

    def out2(ff, sl):
        rows = pl.ds(pl.multiple_of(ff * fc, 8), fc)
        dst = o2.at[rows, :] if layer is None else o2.at[layer, rows, :]
        return pltpu.make_async_copy(acc2.at[sl], dst, out_sem.at[1, sl])

    def wait_out(ff, sl):
        out2(ff, sl).wait()
        if not transpose_out:
            out1(ff, sl).wait()

    @pl.when(step == 0)
    def _():
        start_xg(jnp.int32(0), 0)
        if acc_in is not None:
            for c in in_copies(0, 0):
                c.start()

    @pl.when(step + 1 < nf * nt)
    def _():
        start_xg(jnp.where(t + 1 == nt, 0, t + 1), 1 - slot)

    @pl.when(t == 0)
    def _():
        if acc_in is not None:
            for c in in_copies(f, fs):
                c.wait()
        else:

            @pl.when(f >= 2)
            def _():
                wait_out(f - 2, fs)

            acc1[fs] = jnp.zeros((fc, D), jnp.float32)
            acc2[fs] = jnp.zeros((fc, D), jnp.float32)
        if w1t is not None:
            w1t[...] = w1_ref[...].T

    if acc_in is not None:

        @pl.when((t == 1) & (f + 1 < nf))
        def _():
            @pl.when(f >= 1)
            def _():
                wait_out(f - 1, 1 - fs)

            for c in in_copies(f + 1, 1 - fs):
                c.start()

    wait_xg(slot)

    if n_own:

        @pl.when(t < n_own)
        def _():
            acc2[fs] += dot32(at_ref[...], gb[slot])
            acc1[fs] += dot32(dht_ref[...], xb[slot])

    if n_oth:

        @pl.when(t >= n_own)
        def _():
            left1 = w1t if w1t is not None else w1_ref

            def first(i):
                hs[i] = dot32(left1[...], xb[slot, pl.ds(i * sub, sub), :], NT)
                das[i] = dot32(w2_ref[...], gb[slot, pl.ds(i * sub, sub), :], NT)

            def second(i):
                gelu_out, slope = gelu_pair(hs[i].astype(jnp.bfloat16).astype(jnp.float32))
                ats[i] = gelu_out.astype(jnp.bfloat16)
                dhs[i] = (das[i] * slope).astype(jnp.bfloat16)

            def third(i):
                acc2[fs] += dot32(ats[i], gb[slot, pl.ds(i * sub, sub), :])
                acc1[fs] += dot32(dhs[i], xb[slot, pl.ds(i * sub, sub), :])

            first(0)
            for i in range(nsub):
                if i + 1 < nsub:
                    first(i + 1)
                second(i)
                if i > 0:
                    third(i - 1)
            third(nsub - 1)

    @pl.when(t == nt - 1)
    def _():
        if transpose_out:

            @pl.when(f >= 1)
            def _():
                out1(f - 1, 1 - fs).wait()

            stage[...] = acc1[fs].T
        out1(f, fs).start()
        out2(f, fs).start()

        @pl.when(f == nf - 1)
        def _():
            out1(f, fs).wait()
            out2(f, fs).wait()
            if nf > 1:
                wait_out(f - 1, 1 - fs)


def wgrad(
    q, w1, w2, layer, rows, fc, *, own=None, own_sources=(), sources=(), acc_in=None, tb=1024, sub=512,
    transpose_out=False, w1_transpose=False, out_layer=None, block_mul=0,
):
    nf = rows // fc
    arrays, srcs = [], []

    def index_of(arr):
        for i, known in enumerate(arrays):
            if known is arr:
                return i
        arrays.append(arr)
        return len(arrays) - 1

    for x, xsel, xrow, g, gsel, grow, n in (*own_sources, *sources):
        srcs.append((index_of(x), xsel, xrow, index_of(g), gsel, grow, n))
    n_own = sum(s[-1] for s in own_sources) // tb
    n_oth = sum(s[-1] for s in sources) // tb
    nt = n_own + n_oth
    cfg = dict(
        fc=fc, nf=nf, tb=tb, sub=sub, nt=nt, n_own=n_own, n_oth=n_oth, srcs=srcs, n_arrays=len(arrays),
        acc_in=acc_in is not None, transpose_out=transpose_out, w1_transpose=w1_transpose, out_layer=out_layer,
    )
    block = (lambda f, q_ref: f + block_mul * q_ref[0]) if block_mul else (lambda f, q_ref: f)
    ins, in_specs = [], []
    if n_own:
        spec = pl.BlockSpec((fc, tb), lambda f, t, q_ref: (block(f, q_ref), jnp.minimum(t, n_own - 1)))
        ins += list(own)
        in_specs += [spec, spec]
    if n_oth:
        if w1_transpose:
            in_specs.append(pl.BlockSpec((None, D, fc), lambda f, t, q_ref: (layer, 0, block(f, q_ref))))
        else:
            in_specs.append(pl.BlockSpec((fc, D), lambda f, t, q_ref: (block(f, q_ref), 0)))
        in_specs.append(pl.BlockSpec((None, fc, D), lambda f, t, q_ref: (layer, block(f, q_ref), 0)))
        ins += [w1, w2]
    ins += arrays
    if acc_in is not None:
        ins += list(acc_in)
    in_specs += [ANY] * (len(ins) - len(in_specs))
    scratch = [
        pltpu.VMEM((2, tb, D), jnp.bfloat16),
        pltpu.VMEM((2, tb, D), jnp.bfloat16),
        pltpu.VMEM((2, fc, D), jnp.float32),
        pltpu.VMEM((2, fc, D), jnp.float32),
        pltpu.SemaphoreType.DMA((2, 2)),
        pltpu.SemaphoreType.DMA((2, 2)),
        pltpu.SemaphoreType.DMA((2, 2)),
    ]
    if transpose_out:
        scratch.append(pltpu.VMEM((D, fc), jnp.float32))
    if w1_transpose and n_oth:
        scratch.append(pltpu.VMEM((fc, D), jnp.bfloat16))
    if n_oth:
        nsub = tb // sub
        scratch += [pltpu.VMEM((nsub, fc, sub), jnp.float32)] * 2
        scratch += [pltpu.VMEM((nsub, fc, sub), jnp.bfloat16)] * 2
    if transpose_out:
        shapes = [(2, D, F), (2, F, D)]
    else:
        shapes = [(rows, D), (rows, D)]
    flops = 4 * tb * (n_own + 2 * n_oth) * D * rows
    return pl.pallas_call(
        functools.partial(wgrad_body, cfg),
        grid_spec=pltpu.PrefetchScalarGridSpec(
            num_scalar_prefetch=1, grid=(nf, nt), in_specs=in_specs, out_specs=[ANY] * 2, scratch_shapes=scratch
        ),
        out_shape=[jax.ShapeDtypeStruct(s, jnp.float32) for s in shapes],
        compiler_params=pltpu.CompilerParams(
            dimension_semantics=("arbitrary", "arbitrary"), vmem_limit_bytes=VMEM_LIMIT
        ),
        cost_estimate=pl.CostEstimate(flops=flops, bytes_accessed=16 * rows * D, transcendentals=0),
    )(q, *ins)


def place_body(q_ref, *refs):
    ones, twos = refs[0:4], refs[4:8]
    o1, o2, buf, slots, stage, in_sem, two_in, two_out, out_sem = refs[10:]
    q = q_ref[0]
    fc = stage.shape[2]

    def rows(k):
        return pl.ds(pl.multiple_of(jnp.bitwise_xor(q, k) * QUARTER, 8), QUARTER)

    first = [pltpu.make_async_copy(ones[k], buf.at[rows(k), :], in_sem.at[k]) for k in range(4)]
    for c in first:
        c.start()
    two = [pltpu.make_async_copy(twos[k], slots.at[k % 2], two_in.at[k % 2]) for k in range(4)]
    out = [pltpu.make_async_copy(slots.at[k % 2], o2.at[0, rows(k), :], two_out.at[k % 2]) for k in range(4)]
    two[0].start()
    two[1].start()
    for c in first:
        c.wait()
    done = [
        pltpu.make_async_copy(stage.at[j % 2], o1.at[0, :, pl.ds(j * fc, fc)], out_sem.at[j % 2])
        for j in range(F // fc)
    ]
    for j in range(F // fc):
        if j >= 2:
            done[j - 2].wait()
        stage[j % 2] = buf[pl.ds(j * fc, fc), :].T
        done[j].start()
        if j < 4:
            two[j].wait()
            out[j].start()
            if j >= 1 and j + 1 < 4:
                out[j - 1].wait()
                two[j + 1].start()
    for c in (out[2], out[3], *done[-2:]):
        c.wait()


def place(q, ones, twos, dest):
    return pl.pallas_call(
        place_body,
        grid_spec=pltpu.PrefetchScalarGridSpec(
            num_scalar_prefetch=1,
            grid=(1,),
            in_specs=[ANY] * 10,
            out_specs=[ANY] * 2,
            scratch_shapes=[
                pltpu.VMEM((F, D), jnp.float32),
                pltpu.VMEM((2, QUARTER, D), jnp.float32),
                pltpu.VMEM((2, D, 640), jnp.float32),
                pltpu.SemaphoreType.DMA((4,)),
                pltpu.SemaphoreType.DMA((2,)),
                pltpu.SemaphoreType.DMA((2,)),
                pltpu.SemaphoreType.DMA((2,)),
            ],
        ),
        out_shape=[jax.ShapeDtypeStruct((2, D, F), jnp.float32), jax.ShapeDtypeStruct((2, F, D), jnp.float32)],
        input_output_aliases={9: 0, 10: 1},
        compiler_params=pltpu.CompilerParams(dimension_semantics=("arbitrary",), vmem_limit_bytes=VMEM_LIMIT),
        cost_estimate=pl.CostEstimate(flops=10**9, bytes_accessed=16 * F * D, transcendentals=0),
        name="place",
    )(q, *ones, *twos, *dest)


X_PERM = [(i, i ^ 1) for i in range(4)]
Y_PERM = [(i, i ^ 2) for i in range(4)]
C_PERM = [(0, 1), (1, 0)]


def over_x(a):
    return lax.ppermute(a, "dp", X_PERM)


def over_y(a):
    return lax.ppermute(a, "dp", Y_PERM)


def over_c(a):
    return lax.ppermute(a, "tp", C_PERM)


def after(value, *before):
    return lax.optimization_barrier((value, *before))[0]


def add_parts(grad, own, other):
    total = own.astype(jnp.float32) + other.astype(jnp.float32)
    return (grad.astype(jnp.float32) + total).astype(jnp.bfloat16)


def solution(mesh):
    def backward(w_up, w_down, x_saved, h_saved, grad_out):
        core = lax.axis_index("tp")
        chip = lax.axis_index("dp")
        q_keep = chip.astype(jnp.int32).reshape(1)
        q_send = jnp.bitwise_xor(q_keep, 2)
        zero = jnp.zeros((1,), jnp.int32)

        grad = grad_out[0]

        def half(a, *sel):
            start = (*sel, core * 2048, 0)
            return lax.dynamic_slice(a, start, (1,) * len(sel) + (2048, D)).reshape(2048, D)

        g2h, x0h, x1h = half(grad_out, 0), half(x_saved, 0, 0), half(x_saved, 1, 0)
        g2y, x0x = over_y(g2h), over_x(x0h)
        x1y = over_y(x1h)

        aT1, dHT1, p1 = chain(after(grad, g2h, x0h, x1h), h_saved, w_up, w_down, 1)
        g1 = add_parts(grad, p1, over_c(p1))
        g1h = half(g1)
        g1x = over_x(g1h)
        g2x, x1x = over_x(after(g2h, g1h)), over_x(after(x1h, g1h))
        g2d, x1d = over_y(g2x), over_x(x1y)
        x0x_c, g1x_c = over_c(x0x), over_c(g1x)
        g2y_c, x1y_c = over_c(g2y), over_c(x1y)
        g2x_c, x1x_c = over_c(g2x), over_c(x1x)
        g2d_c, x1d_c = over_c(g2d), over_c(x1d)

        aT0, dHT0, p0, w1t0 = chain(after(g1, g1h), h_saved, w_up, w_down, 0, emit_w1t=True)
        p0_c = over_c(p0)

        own0 = dict(
            own=(aT0, dHT0),
            own_sources=[(x_saved, (0, 0), 0, g1, (), 0, TOKENS)],
            sources=[(x0x, (), 0, g1x, (), 0, 2048), (x0x_c, (), 0, g1x_c, (), 0, 2048)],
            block_mul=2,
        )
        s1, s2 = wgrad(q_send, w1t0, w_down, 0, QUARTER, 560, **own0)
        r1, r2 = over_y(s1), over_y(s2)

        part = wgrad(
            after(zero, s1), w_up, w_down, 1, F, 640, w1_transpose=True, own=(aT1, dHT1),
            own_sources=[(x_saved, (1, 0), 0, grad_out, (0,), 0, TOKENS)],
            sources=[(x1y, (), 0, g2y, (), 0, 2048), (x1y_c, (), 0, g2y_c, (), 0, 2048)],
        )
        f1, f2 = wgrad(after(q_keep, part[0]), w1t0, w_down, 0, QUARTER, 560, acc_in=(r1, r2), **own0)
        f1x, f2y = over_x(f1), over_y(f2)
        f2x, f1y = over_x(f2), over_y(f1)
        f1d, f2d = over_y(f1x), over_x(f2y)
        part = wgrad(
            after(zero, f1), w_up, w_down, 1, F, 640, acc_in=part, w1_transpose=True,
            sources=[(x1x, (), 0, g2x, (), 0, 2048), (x1x_c, (), 0, g2x_c, (), 0, 2048)],
        )
        g0 = add_parts(g1, after(p0, part[0]), p0_c)
        dest = wgrad(
            after(zero, part[0]), w_up, w_down, 1, F, 640, acc_in=part, w1_transpose=True, transpose_out=True,
            out_layer=1,
            sources=[(x1d, (), 0, g2d, (), 0, 2048), (x1d_c, (), 0, g2d_c, (), 0, 2048)],
        )
        up, down = place(q_keep, (f1, f1x, f1y, f1d), (f2, f2x, f2y, f2d), dest)
        return g0[None], up, down

    return jax.shard_map(
        backward,
        mesh=mesh,
        in_specs=(
            P(None, None, "tp"),
            P(None, "tp", None),
            P(None, "dp", None, None),
            P(None, "dp", None, "tp"),
            P("dp", None, None),
        ),
        out_specs=(P("dp", None, None), P(None, None, "tp"), P(None, "tp", None)),
        check_vma=False,
    )
```

time: 2660 us -> 1830 us (0.69)
  waiting for transfers between devices: 1780 us -> 263 us
  Pallas kernels: 0 us -> 1480 us
  matrix products: 670 us -> 0 us
  local copies, waits for them, and re-layouts: 91.7 us -> 23.6 us
  other arithmetic: 92.5 us -> 29.2 us
    psum x3 -> x0, waiting for transfers between devices: 1780 us -> none  [the longest x1 1780 us: run_backward(): lax.psum(jnp.stack([up_grads[layer_idx] for layer_idx in range(layer_coun...]
    pallas_call x0 -> x8, Pallas kernels: none -> 1480 us  [the longest x5 1100 us: wgrad(): pl.pallas_call(functools.partial(wgrad_body, cfg), grid_spec=pltpu.Prefet...]
    dot_general x8 -> x0, matrix products: 670 us -> none  [the longest x2 230 us: run_backward(): jnp.einsum('bsd,fd->bsf', grad_cur, w_down[layer_idx], preferred_element_...]
    ppermute x0 -> x26, waiting for transfers between devices: none -> 263 us  [the longest x8 230 us: over_x(): return lax.ppermute(a, 'dp', X_PERM)]
    unnamed x2, local copies, waits for them, and re-layouts: 91.7 us -> 4.77 us
    another operation x2 -> x0, other arithmetic: 74.7 us -> none  [the longest x1 37.4 us: run_backward(): jnp.stack([up_grads[layer_idx] for layer_idx in range(layer_count)])]
  transfers between devices with their start and end apart: 3 -> 26, of which waited for: 1 -> 6; matrix products, arithmetic and copies ran while one was open for 15% -> 2% of each run, Pallas kernels for 0% -> 70%
where the time goes in v1:
time: 1830 us; the launch traced here: 1820 us
  Pallas kernels  1480 us (81%)
  waiting for transfers between devices  263 us (14%)
  other arithmetic  29.2 us (2%)
  local copies, waits for them, and re-layouts  23.6 us (1%)
  starting transfers between devices  23.2 us (1%)
    pallas_call x5, Pallas kernels, wgrad(): pl.pallas_call(functools.partial(wgrad_body, cfg), grid_spec=pltpu.Prefet...  1100 us
    pallas_call x2, Pallas kernels, chain(): pl.pallas_call(functools.partial(chain_body, sub, nsub, nf, emit_w1t), gr...  347 us
    ppermute x8, waiting for transfers between devices, over_x(): return lax.ppermute(a, 'dp', X_PERM)  230 us
    pallas_call x1, Pallas kernels, place(): pl.pallas_call(place_body, grid_spec=pltpu.PrefetchScalarGridSpec(num_sca...  39.6 us
  transfers between devices with their start and end apart: 26, of which 6 were waited for; matrix products, arithmetic and copies ran while one was open for 2% of the time, Pallas kernels for 70%

profile of v1, /device:TPU:0, one launch (start us, length us, event | category | flops | bytes accessed | tf_op | source)
XLA Modules:
  0.0 1824.7 jit_solution(14140697882427070145)
XLA Ops:
  0.6 10.0 dynamic-slice_bitcast_fusion
  10.7 5.8 dynamic-slice_bitcast_fusion.2
  16.5 170.5 %shard_map.76 = (bf16[4480,4096]{1,0:T(8,128)(2,1)}, bf16[4480,4096]{1,0:T(8,128)(2,1)}, bf16[4096,1536]{1,0:T(8,128)(2,1)}) custom-call(bf16[4096,1536]{1,0:T(8,128)(2,1)} %bitcast.11, bf16[2,1,4096,4480]{3,2,1,0:T(8,128)(2,1)} %h_ref.3, bf16[2,1536,4480]{2,1,0:T(8,128)(2,1)} %refs_1_.3, bf16[2,4480,1536]{2,1,0:T(8,128)(2,1)} %refs_2_.3), custom_call_target="tpu_custom_call" | custom-call | flops 112742891520 | bytes 110100480 | tf_op jit(solution)/shard_map/pallas_call | solution.py:91
  186.9 0.8 collective-permute-start
  187.8 2.5 collective-permute-start.1
  190.3 1.5 collective-permute-start.5
  191.8 15.0 collective-permute-done
  206.8 11.1 add_convert_fusion.1.g_ref.refs_6_
  217.9 0.0 copy-start
  217.9 4.8 copy-done
  222.7 3.0 constant_dynamic-slice_fusion
  225.7 2.8 collective-permute-start.2
  228.5 1.5 collective-permute-start.6
  230.1 96.9 %collective-permute-done.1.refs_7_ = bf16[2048,1536]{1,0:T(8,128)(2,1)} collective-permute-done((bf16[2048,1536]{1,0:T(8,128)(2,1)}, bf16[2048,1536]{1,0:T(8,128)(2,1)}, u32[]{:S(2)}, u32[]{:S(2)}) %collective-permute-start.1) | collective-permute-done | bytes 6291488 | tf_op jit(solution)/shard_map/ppermute | solution.py:418
  327.0 0.0 collective-permute-start.3
  327.0 2.0 collective-permute-done.5.refs_7_
  329.0 0.0 collective-permute-start.7
  329.0 0.5 collective-permute-start.12
  329.5 132.3 %collective-permute-done.2.refs_8_ = bf16[2048,1536]{1,0:T(8,128)(2,1)} collective-permute-done((bf16[2048,1536]{1,0:T(8,128)(2,1)}, bf16[2048,1536]{1,0:T(8,128)(2,1)}, u32[]{:S(2)}, u32[]{:S(2)}) %collective-permute-start.2) | collective-permute-done | bytes 6291488 | tf_op jit(solution)/shard_map/ppermute | solution.py:418
  461.8 0.0 collective-permute-start.4
  461.8 176.0 %shard_map.77 = (bf16[4480,4096]{1,0:T(8,128)(2,1)}, bf16[4480,4096]{1,0:T(8,128)(2,1)}, bf16[4096,1536]{1,0:T(8,128)(2,1)}, bf16[4480,1536]{1,0:T(8,128)(2,1)}) custom-call(bf16[4096,1536]{1,0:T(8,128)(2,1)} %copy-done, bf16[2,1,4096,4480]{3,2,1,0:T(8,128)(2,1)} %h_ref.3, bf16[2,1536,4480]{2,1,0:T(8,128)(2,1)} %refs_1_.3, bf16[2,4480,1536]{2,1,0:T(8,128)(2,1)} %refs_2_.3), custom_call_target="tpu_custom_call" | custom-call | flops 112742891520 | bytes 110100480 | tf_op jit(solution)/shard_map/pallas_call | solution.py:91
  637.8 0.0 collective-permute-done.6.refs_8_
  637.8 2.0 collective-permute-start.22
  639.9 0.0 collective-permute-done.3.refs_9_
  639.9 0.2 collective-permute-start.8
  640.1 0.0 collective-permute-done.12.refs_4_
  640.1 0.3 collective-permute-start.11
  640.4 0.0 collective-permute-done.4.refs_10_
  640.4 1.7 collective-permute-start.23
  642.1 101.1 %shard_map.78 = (f32[1120,1536]{1,0:T(8,128)}, f32[1120,1536]{1,0:T(8,128)}) custom-call(s32[1]{0:T(128)S(6)} %xor.3.refs_0_, bf16[4480,4096]{1,0:T(8,128)(2,1)} %get-tuple-element.35.refs_1_, bf16[4480,4096]{1,0:T(8,128)(2,1)} %get-tuple-element.36.refs_2_, bf16[4480,1536]{1,0:T(8,128)(2,1)} %get-tuple-element.37.refs_3_, bf16[2,4480,1536]{2,1,0:T(8,128)(2,1)} %refs_2_.3, ...), custom_call_target="tpu_custom_call" | custom-call | flops 84557168640 | bytes 27525120 | tf_op jit(solution)/shard_map/pallas_call | solution.py:336
  743.2 0.0 collective-permute-done.7.refs_9_
  743.3 0.3 collective-permute-start.9
  743.6 0.0 collective-permute-done.8.refs_10_
  743.6 1.7 collective-permute-start.10
  745.3 379.3 %shard_map.79 = (f32[4480,1536]{1,0:T(8,128)}, f32[4480,1536]{1,0:T(8,128)}) custom-call(s32[1]{0:T(128)} %constant.7.clone.1.refs_0_, bf16[4480,4096]{1,0:T(8,128)(2,1)} %get-tuple-element.40.refs_1_, bf16[4480,4096]{1,0:T(8,128)(2,1)} %get-tuple-element.41.refs_2_, bf16[2,1536,4480]{2,1,0:T(8,128)(2,1)} %refs_1_.3, bf16[2,4480,1536]{2,1,0:T(8,128)(2,1)} %refs_2_.3, ...), custom_call_target="tpu_custom_call" | custom-call | flops 338228674560 | bytes 110100480 | tf_op jit(solution)/shard_map/pallas_call | solution.py:336
  1124.7 0.0 collective-permute-done.22.refs_3_
  1124.7 0.0 collective-permute-start.15
  1124.7 0.0 collective-permute-done.11.refs_3_
  1124.7 0.5 collective-permute-start.24
  1125.2 0.0 collective-permute-done.23.refs_4_
  1125.2 0.0 collective-permute-start.14
  1125.2 0.0 collective-permute-done.10.refs_12_
  1125.2 0.5 collective-permute-start.13
  1125.7 0.0 collective-permute-done.9.refs_11_
  1125.7 0.0 collective-permute-start.25
  1125.8 105.3 %shard_map.80 = (f32[1120,1536]{1,0:T(8,128)}, f32[1120,1536]{1,0:T(8,128)}) custom-call(s32[1]{0:T(128)} %bitcast.4.refs_0_.q_ref, bf16[4480,4096]{1,0:T(8,128)(2,1)} %get-tuple-element.35.refs_1_, bf16[4480,4096]{1,0:T(8,128)(2,1)} %get-tuple-element.36.refs_2_, bf16[4480,1536]{1,0:T(8,128)(2,1)} %get-tuple-element.37.refs_3_, ...), custom_call_target="tpu_custom_call" | custom-call | flops 84557168640 | bytes 27525120 | tf_op jit(solution)/shard_map/pallas_call | solution.py:336
  1231.1 0.0 collective-permute-done.13.refs_5_
  1231.1 1.5 collective-permute-start.16
  1232.6 0.0 collective-permute-done.14.refs_6_
  1232.6 0.5 collective-permute-start.20
  1233.1 252.5 %shard_map.81 = (f32[4480,1536]{1,0:T(8,128)}, f32[4480,1536]{1,0:T(8,128)}) custom-call(s32[1]{0:T(128)} %constant.7.clone.1.refs_0_, bf16[2,1536,4480]{2,1,0:T(8,128)(2,1)} %refs_1_.3, bf16[2,4480,1536]{2,1,0:T(8,128)(2,1)} %refs_2_.3, bf16[2048,1536]{1,0:T(8,128)(2,1)} %collective-permute-done.11.refs_3_, ...), custom_call_target="tpu_custom_call" | custom-call | flops 225485783040 | bytes 110100480 | tf_op jit(solution)/shard_map/pallas_call | solution.py:336
  1485.6 0.0 collective-permute-done.24.refs_5_
  1485.6 1.5 collective-permute-start.17
  1487.1 0.0 collective-permute-done.25.refs_6_
  1487.1 0.5 collective-permute-start.19
  1487.7 0.3 collective-permute-start.18
  1488.0 0.0 collective-permute-done.20.refs_6_
  1488.0 1.7 collective-permute-start.21
  1489.7 259.7 %shard_map.82 = (f32[2,1536,4480]{2,1,0:T(8,128)}, f32[2,4480,1536]{2,1,0:T(8,128)}) custom-call(s32[1]{0:T(128)} %constant.7.clone.1.refs_0_, bf16[2,1536,4480]{2,1,0:T(8,128)(2,1)} %refs_1_.3, bf16[2,4480,1536]{2,1,0:T(8,128)(2,1)} %refs_2_.3, bf16[2048,1536]{1,0:T(8,128)(2,1)} %collective-permute-done.22.refs_3_, ...), custom_call_target="tpu_custom_call" | custom-call | flops 225485783040 | bytes 110100480 | tf_op jit(solution)/shard_map/pallas_call | solution.py:336
  1749.4 18.0 fusion
  1767.4 0.0 collective-permute-done.19.refs_5_
  1767.4 15.9 collective-permute-done.18.refs_3_
  1783.4 1.2 collective-permute-done.21.refs_7_
  1784.6 39.6 %place.1 = (f32[2,1536,4480]{2,1,0:T(8,128)}, f32[2,4480,1536]{2,1,0:T(8,128)}) custom-call(s32[1]{0:T(128)} %bitcast.4.refs_0_.q_ref, f32[1120,1536]{1,0:T(8,128)} %get-tuple-element.45.refs_0_, f32[1120,1536]{1,0:T(8,128)} %collective-permute-done.16.refs_1_, ...), custom_call_target="tpu_custom_call", output_to_operand_aliasing={{0}: (9, {}), {1}: (10, {})} | custom-call | flops 1000000000 | bytes 110100480 | tf_op jit(solution)/shard_map/place/pallas_call | solution.py:387
  (3 shorter events, 0.0 us)
Async XLA Ops:
  186.9 19.8 %collective-permute-start = (bf16[4096,1536]{1,0:T(8,128)(2,1)}, bf16[4096,1536]{1,0:T(8,128)(2,1)S(1)}, u32[]{:S(2)}, u32[]{:S(2)}) collective-permute-start(bf16[4096,1536]{1,0:T(8,128)(2,1)} %get-tuple-element.32), channel_id=1, source_target_pairs={{0,1},{1,0},{2,3},{3,2},{4,5},{5,4},{6,7},{7,6}} | collective-permute-start | bytes 37748744 | tf_op jit(solution)/shard_map/ppermute | solution.py:426
  187.8 139.2 %collective-permute-start.1 = (bf16[2048,1536]{1,0:T(8,128)(2,1)}, bf16[2048,1536]{1,0:T(8,128)(2,1)}, u32[]{:S(2)}, u32[]{:S(2)}) collective-permute-start(bf16[2048,1536]{1,0:T(8,128)(2,1)} %get-tuple-element.60), channel_id=1, source_target_pairs={{0,2},{2,0},{4,6},{6,4},{1,3},{3,1},{5,7},{7,5}} | collective-permute-start | bytes 18874376 | tf_op jit(solution)/shard_map/ppermute | solution.py:418
  190.3 138.7 %collective-permute-start.5 = (bf16[2048,1536]{1,0:T(8,128)(2,1)}, bf16[2048,1536]{1,0:T(8,128)(2,1)}, u32[]{:S(2)}, u32[]{:S(2)}) collective-permute-start(bf16[2048,1536]{1,0:T(8,128)(2,1)} %get-tuple-element.47), channel_id=1, source_target_pairs={{0,4},{2,6},{4,0},{6,2},{1,5},{3,7},{5,1},{7,3}} | collective-permute-start | bytes 18874376 | tf_op jit(solution)/shard_map/ppermute | solution.py:422
  217.9 4.8 copy-start
  225.7 236.1 %collective-permute-start.2 = (bf16[2048,1536]{1,0:T(8,128)(2,1)}, bf16[2048,1536]{1,0:T(8,128)(2,1)}, u32[]{:S(2)}, u32[]{:S(2)}) collective-permute-start(bf16[2048,1536]{1,0:T(8,128)(2,1)} %constant_dynamic-slice_fusion), channel_id=1, source_target_pairs={{0,2},{2,0},{4,6},{6,4},{1,3},{3,1},{5,7},{7,5}} | collective-permute-start | bytes 18874376 | tf_op jit(solution)/shard_map/ppermute | solution.py:418
  228.5 409.3 %collective-permute-start.6 = (bf16[2048,1536]{1,0:T(8,128)(2,1)}, bf16[2048,1536]{1,0:T(8,128)(2,1)}, u32[]{:S(2)}, u32[]{:S(2)}) collective-permute-start(bf16[2048,1536]{1,0:T(8,128)(2,1)} %dynamic-slice_bitcast_fusion.2), channel_id=1, source_target_pairs={{0,4},{2,6},{4,0},{6,2},{1,5},{3,7},{5,1},{7,3}} | collective-permute-start | bytes 18874376 | tf_op jit(solution)/shard_map/ppermute | solution.py:422
  327.0 312.9 %collective-permute-start.3 = (bf16[2048,1536]{1,0:T(8,128)(2,1)}, bf16[2048,1536]{1,0:T(8,128)(2,1)}, u32[]{:S(2)}, u32[]{:S(2)}) collective-permute-start(bf16[2048,1536]{1,0:T(8,128)(2,1)} %collective-permute-done.1.refs_7_), channel_id=1, source_target_pairs={{0,1},{1,0},{2,3},{3,2},{4,5},{5,4},{6,7},{7,6}} | collective-permute-start | bytes 18874376 | tf_op jit(solution)/shard_map/ppermute | solution.py:426
  329.0 414.3 %collective-permute-start.7 = (bf16[2048,1536]{1,0:T(8,128)(2,1)}, bf16[2048,1536]{1,0:T(8,128)(2,1)}, u32[]{:S(2)}, u32[]{:S(2)}) collective-permute-start(bf16[2048,1536]{1,0:T(8,128)(2,1)} %collective-permute-done.5.refs_7_), channel_id=1, source_target_pairs={{0,1},{1,0},{2,3},{3,2},{4,5},{5,4},{6,7},{7,6}} | collective-permute-start | bytes 18874376 | tf_op jit(solution)/shard_map/ppermute | solution.py:426
  329.0 311.1 %collective-permute-start.12 = (bf16[2048,1536]{1,0:T(8,128)(2,1)}, bf16[2048,1536]{1,0:T(8,128)(2,1)}, u32[]{:S(2)}, u32[]{:S(2)}) collective-permute-start(bf16[2048,1536]{1,0:T(8,128)(2,1)} %dynamic-slice_bitcast_fusion.2), channel_id=1, source_target_pairs={{0,2},{2,0},{4,6},{6,4},{1,3},{3,1},{5,7},{7,5}} | collective-permute-start | bytes 18874376 | tf_op jit(solution)/shard_map/ppermute | solution.py:418
  461.8 178.6 %collective-permute-start.4 = (bf16[2048,1536]{1,0:T(8,128)(2,1)}, bf16[2048,1536]{1,0:T(8,128)(2,1)}, u32[]{:S(2)}, u32[]{:S(2)}) collective-permute-start(bf16[2048,1536]{1,0:T(8,128)(2,1)} %collective-permute-done.2.refs_8_), channel_id=1, source_target_pairs={{0,1},{1,0},{2,3},{3,2},{4,5},{5,4},{6,7},{7,6}} | collective-permute-start | bytes 18874376 | tf_op jit(solution)/shard_map/ppermute | solution.py:426
  637.8 486.8 %collective-permute-start.22 = (bf16[2048,1536]{1,0:T(8,128)(2,1)}, bf16[2048,1536]{1,0:T(8,128)(2,1)}, u32[]{:S(2)}, u32[]{:S(2)}) collective-permute-start(bf16[2048,1536]{1,0:T(8,128)(2,1)} %collective-permute-done.5.refs_7_), channel_id=1, source_target_pairs={{0,2},{2,0},{4,6},{6,4},{1,3},{3,1},{5,7},{7,5}} | collective-permute-start | bytes 18874376 | tf_op jit(solution)/shard_map/ppermute | solution.py:418
  639.9 103.7 %collective-permute-start.8 = (bf16[2048,1536]{1,0:T(8,128)(2,1)}, bf16[2048,1536]{1,0:T(8,128)(2,1)}, u32[]{:S(2)}, u32[]{:S(2)}) collective-permute-start(bf16[2048,1536]{1,0:T(8,128)(2,1)} %collective-permute-done.6.refs_8_), channel_id=1, source_target_pairs={{0,1},{1,0},{2,3},{3,2},{4,5},{5,4},{6,7},{7,6}} | collective-permute-start | bytes 18874376 | tf_op jit(solution)/shard_map/ppermute | solution.py:426
  640.1 484.6 %collective-permute-start.11 = (bf16[2048,1536]{1,0:T(8,128)(2,1)}, bf16[2048,1536]{1,0:T(8,128)(2,1)}, u32[]{:S(2)}, u32[]{:S(2)}) collective-permute-start(bf16[2048,1536]{1,0:T(8,128)(2,1)} %get-tuple-element.47), channel_id=1, source_target_pairs={{0,2},{2,0},{4,6},{6,4},{1,3},{3,1},{5,7},{7,5}} | collective-permute-start | bytes 18874376 | tf_op jit(solution)/shard_map/ppermute | solution.py:418
  640.4 484.8 %collective-permute-start.23 = (bf16[2048,1536]{1,0:T(8,128)(2,1)}, bf16[2048,1536]{1,0:T(8,128)(2,1)}, u32[]{:S(2)}, u32[]{:S(2)}) collective-permute-start(bf16[2048,1536]{1,0:T(8,128)(2,1)} %collective-permute-done.12.refs_4_), channel_id=1, source_target_pairs={{0,4},{2,6},{4,0},{6,2},{1,5},{3,7},{5,1},{7,3}} | collective-permute-start | bytes 18874376 | tf_op jit(solution)/shard_map/ppermute | solution.py:422
  743.3 382.5 %collective-permute-start.9 = (f32[1120,1536]{1,0:T(8,128)}, f32[1120,1536]{1,0:T(8,128)}, u32[]{:S(2)}, u32[]{:S(2)}) collective-permute-start(f32[1120,1536]{1,0:T(8,128)} %get-tuple-element.38), channel_id=1, source_target_pairs={{0,4},{2,6},{4,0},{6,2},{1,5},{3,7},{5,1},{7,3}} | collective-permute-start | bytes 20643848 | tf_op jit(solution)/shard_map/ppermute | solution.py:422
  743.6 381.7 %collective-permute-start.10 = (f32[1120,1536]{1,0:T(8,128)}, f32[1120,1536]{1,0:T(8,128)}, u32[]{:S(2)}, u32[]{:S(2)}) collective-permute-start(f32[1120,1536]{1,0:T(8,128)} %get-tuple-element.44), channel_id=1, source_target_pairs={{0,4},{2,6},{4,0},{6,2},{1,5},{3,7},{5,1},{7,3}} | collective-permute-start | bytes 20643848 | tf_op jit(solution)/shard_map/ppermute | solution.py:422
  1124.7 624.7 %collective-permute-start.15 = (bf16[4096,1536]{1,0:T(8,128)(2,1)}, bf16[4096,1536]{1,0:T(8,128)(2,1)}, u32[]{:S(2)}, u32[]{:S(2)}) collective-permute-start(bf16[4096,1536]{1,0:T(8,128)(2,1)} %get-tuple-element.51), channel_id=1, source_target_pairs={{0,1},{1,0},{2,3},{3,2},{4,5},{5,4},{6,7},{7,6}} | collective-permute-start | bytes 37748744 | tf_op jit(solution)/shard_map/ppermute | solution.py:426
  1124.7 360.9 %collective-permute-start.24 = (bf16[2048,1536]{1,0:T(8,128)(2,1)}, bf16[2048,1536]{1,0:T(8,128)(2,1)}, u32[]{:S(2)}, u32[]{:S(2)}) collective-permute-start(bf16[2048,1536]{1,0:T(8,128)(2,1)} %collective-permute-done.22.refs_3_), channel_id=1, source_target_pairs={{0,1},{1,0},{2,3},{3,2},{4,5},{5,4},{6,7},{7,6}} | collective-permute-start | bytes 18874376 | tf_op jit(solution)/shard_map/ppermute | solution.py:426
  1125.2 107.4 %collective-permute-start.14 = (bf16[2048,1536]{1,0:T(8,128)(2,1)}, bf16[2048,1536]{1,0:T(8,128)(2,1)}, u32[]{:S(2)}, u32[]{:S(2)}) collective-permute-start(bf16[2048,1536]{1,0:T(8,128)(2,1)} %collective-permute-done.12.refs_4_), channel_id=1, source_target_pairs={{0,1},{1,0},{2,3},{3,2},{4,5},{5,4},{6,7},{7,6}} | collective-permute-start | bytes 18874376 | tf_op jit(solution)/shard_map/ppermute | solution.py:426
  1125.2 105.8 %collective-permute-start.13 = (bf16[2048,1536]{1,0:T(8,128)(2,1)}, bf16[2048,1536]{1,0:T(8,128)(2,1)}, u32[]{:S(2)}, u32[]{:S(2)}) collective-permute-start(bf16[2048,1536]{1,0:T(8,128)(2,1)} %collective-permute-done.11.refs_3_), channel_id=1, source_target_pairs={{0,1},{1,0},{2,3},{3,2},{4,5},{5,4},{6,7},{7,6}} | collective-permute-start | bytes 18874376 | tf_op jit(solution)/shard_map/ppermute | solution.py:426
  1125.7 361.4 %collective-permute-start.25 = (bf16[2048,1536]{1,0:T(8,128)(2,1)}, bf16[2048,1536]{1,0:T(8,128)(2,1)}, u32[]{:S(2)}, u32[]{:S(2)}) collective-permute-start(bf16[2048,1536]{1,0:T(8,128)(2,1)} %collective-permute-done.23.refs_4_), channel_id=1, source_target_pairs={{0,1},{1,0},{2,3},{3,2},{4,5},{5,4},{6,7},{7,6}} | collective-permute-start | bytes 18874376 | tf_op jit(solution)/shard_map/ppermute | solution.py:426
  1231.1 256.6 %collective-permute-start.16 = (f32[1120,1536]{1,0:T(8,128)}, f32[1120,1536]{1,0:T(8,128)}, u32[]{:S(2)}, u32[]{:S(2)}) collective-permute-start(f32[1120,1536]{1,0:T(8,128)} %get-tuple-element.45.refs_0_), channel_id=1, source_target_pairs={{0,2},{2,0},{4,6},{6,4},{1,3},{3,1},{5,7},{7,5}} | collective-permute-start | bytes 20643848 | tf_op jit(solution)/shard_map/ppermute | solution.py:418
  1232.6 255.4 %collective-permute-start.20 = (f32[1120,1536]{1,0:T(8,128)}, f32[1120,1536]{1,0:T(8,128)}, u32[]{:S(2)}, u32[]{:S(2)}) collective-permute-start(f32[1120,1536]{1,0:T(8,128)} %get-tuple-element.52.refs_4_), channel_id=1, source_target_pairs={{0,4},{2,6},{4,0},{6,2},{1,5},{3,7},{5,1},{7,3}} | collective-permute-start | bytes 20643848 | tf_op jit(solution)/shard_map/ppermute | solution.py:422
  1485.6 281.8 %collective-permute-start.17 = (f32[1120,1536]{1,0:T(8,128)}, f32[1120,1536]{1,0:T(8,128)}, u32[]{:S(2)}, u32[]{:S(2)}) collective-permute-start(f32[1120,1536]{1,0:T(8,128)} %get-tuple-element.45.refs_0_), channel_id=1, source_target_pairs={{0,4},{2,6},{4,0},{6,2},{1,5},{3,7},{5,1},{7,3}} | collective-permute-start | bytes 20643848 | tf_op jit(solution)/shard_map/ppermute | solution.py:422
  1487.1 280.3 %collective-permute-start.19 = (f32[1120,1536]{1,0:T(8,128)}, f32[1120,1536]{1,0:T(8,128)}, u32[]{:S(2)}, u32[]{:S(2)}) collective-permute-start(f32[1120,1536]{1,0:T(8,128)} %get-tuple-element.52.refs_4_), channel_id=1, source_target_pairs={{0,2},{2,0},{4,6},{6,4},{1,3},{3,1},{5,7},{7,5}} | collective-permute-start | bytes 20643848 | tf_op jit(solution)/shard_map/ppermute | solution.py:418
  1487.7 295.7 %collective-permute-start.18 = (f32[1120,1536]{1,0:T(8,128)}, f32[1120,1536]{1,0:T(8,128)}, u32[]{:S(2)}, u32[]{:S(2)}) collective-permute-start(f32[1120,1536]{1,0:T(8,128)} %collective-permute-done.16.refs_1_), channel_id=1, source_target_pairs={{0,4},{2,6},{4,0},{6,2},{1,5},{3,7},{5,1},{7,3}} | collective-permute-start | bytes 20643848 | tf_op jit(solution)/shard_map/ppermute | solution.py:422
  1488.0 296.6 %collective-permute-start.21 = (f32[1120,1536]{1,0:T(8,128)}, f32[1120,1536]{1,0:T(8,128)}, u32[]{:S(2)}, u32[]{:S(2)}) collective-permute-start(f32[1120,1536]{1,0:T(8,128)} %collective-permute-done.20.refs_6_), channel_id=1, source_target_pairs={{0,2},{2,0},{4,6},{6,4},{1,3},{3,1},{5,7},{7,5}} | collective-permute-start | bytes 20643848 | tf_op jit(solution)/shard_map/ppermute | solution.py:418
